TPU v7x, 32 devices: a whole 2x2x4 slice. The times are simulated.
32 devices in a mesh: dp: 2 (over x), fsdp: 4 (over y, core), tensor: 4 (over z).
Axes of the slice: x: 2, y: 2, z: 4, core: 2. Of those that a mesh axis runs over, the one named last changes fastest.
Arguments:
- hidden: bfloat16 [4096, 2048], P(('dp', 'fsdp'), 'tensor'), may hold values from -8 to 8
- norm_gain: bfloat16 [2048], P('tensor'), may hold values from 0.099609375 to 1.8984375
- head_weight: bfloat16 [2048, 32128], P('fsdp', 'tensor'), may hold values from -1 to 1
- token_ids: int32 [8, 512], P(('dp', 'fsdp')), may hold values from 0 to 32127
- lengths: int32 [8], P(('dp', 'fsdp')), may hold values from 128 to 512
- old_logp: float32 [8, 512], P(('dp', 'fsdp')), may hold values from -12.5 to -9.5
- advantages: float32 [8, 512], P(('dp', 'fsdp')), may hold values from -4 to 4
- rollout_logp: float32 [8, 512], P(('dp', 'fsdp'), 'tensor'), may hold values from -16 to -1
- rollout_row: int32 [8], P(('dp', 'fsdp')), may hold values from 0 to 7, each once
Outputs:
- new_logp: float32 [8, 512], P(('dp', 'fsdp'))
- token_loss: float32 [8, 512], P(('dp', 'fsdp'))
- summary: float32 [3], replicated
Inputs may be any that keep to these rules, and one draw needn't show every extreme that they name: `rollout_row`: every row 0 to 7 is named once.
All inputs are finite; a program needn't handle non-finite values.
Results may differ from a plain program's by a relative error of at most 0.0005.
The roundings to bfloat16 on the way count: a program that leaves them out, or rounds other values in their place, can miss the bound.
Values may be sent and summed in bfloat16 or wider, within the bound.
A program may use at most 128 MiB of HBM per device.

v0:
```python
import jax
import jax.numpy as jnp
from jax import lax
from jax.sharding import PartitionSpec as P

clip_eps = 0.2
kl_coef = 0.2
log_limit = 10.0
norm_eps = 1e-06


def combined_all(value, axis, join):
    pieces = jax.tree.map(lambda part: lax.all_gather(part, axis), value)
    head = jax.tree.map(lambda part: part[0], pieces)
    tail = jax.tree.map(lambda part: part[1:], pieces)
    so_far, _ = lax.scan(lambda so_far, section: (join(so_far, section), None), head, tail)
    return so_far


def token_terms(new_logp, old_logp, advantages, ref_logp, live_mask, prob_square):
    shift = new_logp - old_logp
    prob_ratio = jnp.exp(jnp.clip(shift, -log_limit, log_limit))
    clipped = jnp.clip(prob_ratio, 1.0 - clip_eps, 1.0 + clip_eps)
    plain_term = prob_ratio * advantages
    bounded_term = clipped * advantages
    surrogate = jnp.minimum(plain_term, bounded_term)
    ref_gap = ref_logp - new_logp
    gap_clip = jnp.clip(ref_gap, -log_limit, log_limit)
    kl_term = jnp.exp(gap_clip) - gap_clip - 1.0
    token_loss = live_mask * (kl_coef * kl_term - surrogate)
    inside_gap = (jnp.abs(ref_gap) < log_limit).astype(jnp.float32)
    inside_ratio = (jnp.abs(shift) < log_limit).astype(jnp.float32)
    active_term = (plain_term <= bounded_term).astype(jnp.float32)
    grad_coef = live_mask * (
        kl_coef * (1.0 - jnp.exp(gap_clip)) * inside_gap
        - advantages * prob_ratio * active_term * inside_ratio
    )
    grad_square = grad_coef * grad_coef * (prob_square - 2.0 * jnp.exp(new_logp) + 1.0)
    return (token_loss, live_mask * kl_term, grad_square)


def join_stats(earlier, later):
    row_max = jnp.maximum(earlier[0], later[0])
    left_scale = jnp.exp(earlier[0] - row_max)
    right_scale = jnp.exp(later[0] - row_max)
    exp_sum = earlier[1] * left_scale + later[1] * right_scale
    exp_square = earlier[2] * left_scale * left_scale + later[2] * right_scale * right_scale
    return (row_max, exp_sum, exp_square, earlier[3] + later[3])


def exp_sums(logits, row_max):
    shifted = jnp.exp(logits - row_max[:, None])
    return (jnp.sum(shifted, axis=1), jnp.sum(shifted * shifted, axis=1))


def vocab_stats(logits, flat_ids, col_start):
    col_ids = lax.broadcasted_iota(jnp.int32, logits.shape, 1) + col_start
    picked = jnp.sum(jnp.where(col_ids == flat_ids[:, None], logits, 0.0), axis=1)
    local_max = jnp.max(logits, axis=1)
    row_max = lax.pmax(local_max, "tensor")
    exp_sum, exp_square = exp_sums(logits, row_max)
    exp_sum, exp_square, picked = lax.psum((exp_sum, exp_square, picked), "tensor")
    return (row_max, exp_sum, exp_square, picked)


def shards(
    hidden,
    norm_gain,
    head_weight,
    token_ids,
    lengths,
    old_logp,
    advantages,
    rollout_logp,
    rollout_row,
):
    tok_rows = hidden.shape[0]
    full_rows, full_gain = (
        lax.all_gather(hidden, "tensor", axis=1, tiled=True),
        lax.all_gather(norm_gain, "tensor", axis=0, tiled=True),
    )
    values = full_rows.astype(jnp.float32)
    inv_rms = lax.rsqrt(jnp.mean(values * values, axis=1, keepdims=True) + norm_eps)
    normed = (values * inv_rms * full_gain.astype(jnp.float32)[None, :]).astype(jnp.bfloat16)
    flat_ids = token_ids.reshape(-1)
    vocab_cols = head_weight.shape[1]
    tensor_pos = lax.axis_index("tensor")
    half_cols = vocab_cols // 2
    dp_pos = lax.axis_index("dp")
    own_cols = lax.dynamic_slice_in_dim(head_weight, dp_pos * half_cols, half_cols, 1)
    pair_rows = lax.all_gather(normed, "dp", axis=0, tiled=True)
    pair_ids = lax.all_gather(flat_ids, "dp", axis=0, tiled=True)
    logits = jnp.dot(
        pair_rows,
        lax.all_gather(own_cols, "fsdp", axis=0, tiled=True),
        preferred_element_type=jnp.float32,
    )
    soft_stats = vocab_stats(logits, pair_ids, tensor_pos * vocab_cols + dp_pos * half_cols)
    soft_stats = combined_all(soft_stats, "dp", join_stats)
    soft_stats = tuple(
        (lax.dynamic_slice_in_dim(member, dp_pos * tok_rows, tok_rows, 0) for member in soft_stats)
    )
    row_max, exp_sum, exp_square, picked = soft_stats
    new_logp = (picked - row_max - jnp.log(exp_sum)).reshape(token_ids.shape)
    prob_square = (exp_square / (exp_sum * exp_sum)).reshape(token_ids.shape)
    ref_all = lax.all_gather(rollout_logp, ("dp", "fsdp"), axis=0, tiled=True)
    own_ref = jnp.take(ref_all, rollout_row, axis=0)
    ref_logp = lax.all_gather(own_ref, "tensor", axis=1, tiled=True)
    positions = lax.broadcasted_iota(jnp.int32, token_ids.shape, 1)
    live_mask = (positions < lengths[:, None]).astype(jnp.float32)
    token_loss, kl_part, grad_part = token_terms(
        new_logp, old_logp, advantages, ref_logp, live_mask, prob_square
    )
    live_count, loss_sum, kl_sum, grad_sum = lax.psum(
        (jnp.sum(live_mask), jnp.sum(token_loss), jnp.sum(kl_part), jnp.sum(grad_part)),
        ("dp", "fsdp"),
    )
    summary = jnp.stack(
        [loss_sum / live_count, kl_sum / live_count, jnp.sqrt(grad_sum / live_count)]
    )
    return (new_logp, token_loss, summary)


def solution(mesh):
    in_specs = (
        P(("dp", "fsdp"), "tensor"),
        P("tensor"),
        P("fsdp", "tensor"),
        P(("dp", "fsdp"), None),
        P(("dp", "fsdp")),
        P(("dp", "fsdp"), None),
        P(("dp", "fsdp"), None),
        P(("dp", "fsdp"), "tensor"),
        P(("dp", "fsdp")),
    )
    out_specs = (P(("dp", "fsdp"), None), P(("dp", "fsdp"), None), P())
    return jax.shard_map(shards, mesh=mesh, in_specs=in_specs, out_specs=out_specs, check_vma=False)
```

profile of v0, /device:TPU:0, one launch (start us, length us, event | category | flops | bytes accessed | tf_op | source)
XLA Modules:
  0.0 327.2 jit_solution(12771580866404278968)
XLA Ops:
  7.2 0.7 all-gather.11.cloned.1.call-update
  7.9 0.7 reshape.90
  8.6 13.6 %all-gather.2 = bf16[4,1,512]{2,1,0:T(2,128)(2,1)S(1)} all-gather(bf16[1,1,512]{2,1,0:T(2,128)(2,1)S(1)} %reshape.90), channel_id=1, replica_groups=mesh['dp'=2,'fsdp'=4,'tensor'=4] {'tensor'}, dimensions={0}, use_global_device_ids=true | all-gather | bytes 5120 | tf_op jit(solution)/shard_map/all_gather | solution.py:80
  22.3 35.7 %all-gather.11.cloned.1.call-done = bf16[512,2048]{1,0:T(8,128)(2,1)} async-done(((bf16[512,512]{1,0:T(8,128)(2,1)}), bf16[512,2048]{1,0:T(8,128)(2,1)}) %all-gather.11.cloned.1.call-update) | async-done | bytes 2097168 | tf_op jit(solution)/shard_map/all_gather | solution.py:79
  58.0 2.1 fusion.1
  60.0 3.5 %fusion.3 = bf16[512,2048]{1,0:T(8,128)(2,1)} fusion(bf16[512,2048]{1,0:T(8,128)(2,1)} %all-gather.11.cloned.1.call-done, f32[2048]{0:T(1024)S(1)} %bitcast.29, f32[512]{0:T(512)S(1)} %add_rsqrt_fusion), kind=kLoop, calls=%fused_computation.8 | loop fusion | flops 4194304 | bytes 4204544 | tf_op jit(solution)/shard_map/convert_element_type | solution.py:84
  63.6 4.4 %constant_dynamic-slice_fusion.1 = bf16[512,4016]{0,1:T(8,128)(2,1)} fusion(bf16[512,8032]{0,1:T(8,128)(2,1)} %param.11, s32[]{:T(128)S(6)} %select_n.30), kind=kLoop, calls=%fused_computation.37 | loop fusion | bytes 8224772 | tf_op jit(solution)/shard_map/dynamic_slice | solution.py:90
  69.3 0.6 convert_reduce_fusion
  70.0 8.9 %all-gather.5 = f32[8,1,128]{2,1,0:T(1,128)S(1)} all-gather(f32[1,1,128]{2,1,0:T(1,128)S(1)} %bitcast.45), channel_id=1, replica_groups=mesh['dp'=2,'fsdp'=4,'tensor'=4] {'dp','fsdp'}, dimensions={0}, use_global_device_ids=true | all-gather | bytes 4608 | tf_op jit(solution)/shard_map/all_gather | solution.py:106
  78.8 8.6 %all_gather.57 = f32[1,512]{1,0:T(1,128)S(1)} all-gather(f32[1,128]{1,0:T(1,128)S(1)} %fusion.8), channel_id=1, replica_groups=mesh['dp'=2,'fsdp'=4,'tensor'=4] {'tensor'}, dimensions={1}, use_global_device_ids=true | all-gather | bytes 2560 | tf_op jit(solution)/shard_map/all_gather | solution.py:108
  87.4 4.5 %all-gather = s32[1,1024]{1,0:T(1,128)S(1)} all-gather(s32[1,512]{1,0:T(1,128)S(1)} %copy-done.1), channel_id=2, replica_groups=mesh['dp'=2,'fsdp'=4,'tensor'=4] {'dp'}, dimensions={1}, use_global_device_ids=true | all-gather | bytes 6144 | tf_op jit(solution)/shard_map/all_gather | solution.py:92
  92.0 27.3 %all-gather.13.cloned.1.call-done = bf16[1024,2048]{1,0:T(8,128)(2,1)} async-done(((bf16[512,2048]{1,0:T(8,128)(2,1)}), bf16[1024,2048]{1,0:T(8,128)(2,1)}) %all-gather.13.cloned.1.call-update) | async-done | bytes 4194320 | tf_op jit(solution)/shard_map/all_gather | solution.py:91
  119.3 105.6 %all-gather.15.cloned.1.call-done = bf16[2048,4016]{0,1:T(8,128)(2,1)} async-done(((bf16[512,4016]{0,1:T(8,128)(2,1)}), bf16[2048,4016]{0,1:T(8,128)(2,1)}) %all-gather.15.cloned.1.call-update) | async-done | bytes 16449552 | tf_op jit(solution)/shard_map/all_gather | solution.py:95
  224.9 23.4 %fusion.15 = (f32[1024]{0:T(1024)S(1)}, f32[1024,4016]{0,1:T(8,128)}) fusion(bf16[1024,2048]{1,0:T(8,128)(2,1)} %all-gather.13.cloned.1.call-done, bf16[2048,4016]{0,1:T(8,128)(2,1)} %all-gather.15.cloned.1.call-done), kind=kOutput, calls=%fused_computation.46 | convolution fusion | flops 16848436224 | bytes 37097472 | tf_op jit(solution)/shard_map/dot_general | solution.py:93
  248.3 11.7 %pmax.7 = f32[1024]{0:T(1024)S(1)} all-reduce(f32[1024]{0:T(1024)S(1)} %get-tuple-element.65), channel_id=1, replica_groups=mesh['dp'=2,'fsdp'=4,'tensor'=4] {'tensor'}, use_global_device_ids=true, to_apply=%region_4.5 | all-reduce | flops 1024 | bytes 8192 | tf_op jit(solution)/shard_map/pmax | solution.py:60
  259.9 4.3 %all-gather.1 = f32[2048]{0:T(1024)S(1)} all-gather(f32[1024]{0:T(1024)S(1)} %pmax.7), channel_id=3, replica_groups=mesh['dp'=2,'fsdp'=4,'tensor'=4] {'dp'}, dimensions={0}, use_global_device_ids=true | all-gather | bytes 12288 | tf_op jit(solution)/shard_map/all_gather | solution.py:13
  264.3 8.7 %multiply_reduce_fusion = (f32[1024]{0:T(1024)S(1)}, f32[1024]{0:T(1024)S(1)}, f32[1024]{0:T(1024)S(1)}) fusion(f32[1024,4016]{0,1:T(8,128)} %get-tuple-element.66, f32[1024]{0:T(1024)S(1)} %pmax.7, s32[1024]{0:T(1024)S(1)} %bitcast.33, s32[4016]{0:T(1024)S(1)} %iota_add_fusion), kind=kLoop, calls=%fused_computation | loop fusion | flops 28783616 | bytes 16486080 | tf_op jit(solution)/shard_map/reduce_sum | solution.py:53
  273.0 15.5 %all-reduce.1 = (f32[1,1024]{1,0:T(1,128)S(1)}, f32[1,1024]{1,0:T(1,128)S(1)}, f32[1,1024]{1,0:T(1,128)S(1)}) all-reduce(f32[1,1024]{1,0:T(1,128)S(1)} %bitcast.32, f32[1,1024]{1,0:T(1,128)S(1)} %bitcast.31, f32[1,1024]{1,0:T(1,128)S(1)} %bitcast.30), channel_id=1, replica_groups=mesh['dp'=2,'fsdp'=4,'tensor'=4] {'tensor'}, use_global_device_ids=true, to_apply=%region_2.3 | all-reduce | flops 3072 | bytes 24576 | tf_op jit(solution)/shard_map/psum | solution.py:62
  288.5 4.3 %all-gather.3 = f32[2,1,1024]{2,1,0:T(1,128)S(1)} all-gather(f32[1,1,1024]{2,1,0:T(1,128)S(1)} %bitcast.44), channel_id=1, replica_groups=mesh['dp'=2,'fsdp'=4,'tensor'=4] {'dp'}, dimensions={0}, use_global_device_ids=true | all-gather | bytes 12288 | tf_op jit(solution)/shard_map/all_gather | solution.py:13
  292.9 4.3 %all-gather.6 = f32[2,1,1024]{2,1,0:T(1,128)S(1)} all-gather(f32[1,1,1024]{2,1,0:T(1,128)S(1)} %bitcast.43), channel_id=1, replica_groups=mesh['dp'=2,'fsdp'=4,'tensor'=4] {'dp'}, dimensions={0}, use_global_device_ids=true | all-gather | bytes 12288 | tf_op jit(solution)/shard_map/all_gather | solution.py:13
  297.2 4.3 %all-gather.4 = f32[2,1,1024]{2,1,0:T(1,128)S(1)} all-gather(f32[1,1,1024]{2,1,0:T(1,128)S(1)} %bitcast.42), channel_id=1, replica_groups=mesh['dp'=2,'fsdp'=4,'tensor'=4] {'dp'}, dimensions={0}, use_global_device_ids=true | all-gather | bytes 12288 | tf_op jit(solution)/shard_map/all_gather | solution.py:13
  301.7 1.3 fusion.10
  303.0 0.7 select_reduce_fusion.1
  303.7 12.5 %all-reduce = (f32[]{:T(128)}, f32[]{:T(128)}, f32[]{:T(128)}, f32[]{:T(128)}) all-reduce(f32[]{:T(128)} %get-tuple-element.58, f32[]{:T(128)} %convert_reduce_fusion, f32[]{:T(128)} %select_reduce_fusion.1, f32[]{:T(128)} %get-tuple-element.51), channel_id=1, replica_groups=mesh['dp'=2,'fsdp'=4,'tensor'=4] {'dp','fsdp'}, use_global_device_ids=true, to_apply=%region_16.17 | all-reduce | flops 4 | bytes 32 | tf_op jit(solution)/shard_map/psum | solution.py:114
  (27 shorter events, 0.9 us)
Async XLA Ops:
  7.2 50.8 %all-gather.11.cloned.1.call-start = ((), (), s32[]{:S(2)}) async-start(), calls=%async_computation | async-start | bytes 2621440 | tf_op jit(solution)/shard_map/all_gather | solution.py:79
  7.9 111.4 %all-gather.13.cloned.1.call-start = ((), (), s32[]{:S(2)}) async-start(), calls=%async_computation.1 | async-start | bytes 6291456 | tf_op jit(solution)/shard_map/all_gather | solution.py:91
  63.5 161.4 %all-gather.15.cloned.1.call-start = ((), (), s32[]{:S(2)}) async-start(), calls=%async_computation.2 | async-start | bytes 20561920 | tf_op jit(solution)/shard_map/all_gather | solution.py:95
  63.6 6.4 %copy-start.4 = (f32[1,128]{1,0:T(1,128)S(1)}, f32[1,128]{1,0:T(1,128)}, u32[]{:S(2)}) copy-start(f32[1,128]{1,0:T(1,128)} %param.16) | copy-start | bytes 1540
  63.6 23.8 %copy-start.1 = (s32[1,512]{1,0:T(1,128)S(1)}, s32[1,512]{1,0:T(1,128)}, u32[]{:S(2)}) copy-start(s32[1,512]{1,0:T(1,128)} %param.12) | copy-start | bytes 6148
  264.3 37.4 %copy-start.2 = (f32[1,512]{1,0:T(1,128)S(1)}, f32[1,512]{1,0:T(1,128)}, u32[]{:S(2)}) copy-start(f32[1,512]{1,0:T(1,128)} %param.15) | copy-start | bytes 6148
  264.3 37.4 %copy-start.3 = (f32[1,512]{1,0:T(1,128)S(1)}, f32[1,512]{1,0:T(1,128)}, u32[]{:S(2)}) copy-start(f32[1,512]{1,0:T(1,128)} %param.14) | copy-start | bytes 6148
  301.7 19.0 %copy-start = (f32[512]{0:T(512)}, f32[512]{0:T(512)S(1)}, u32[]{:S(2)}) copy-start(f32[512]{0:T(512)S(1)} %get-tuple-element.55) | copy-start | bytes 6148
Sparse Core Ops, SparseCore 0:
  9.5 48.3 all-gather.10
  63.7 55.5 all-gather.12
  120.9 104.0 all-gather.14
where the time goes:
time: 328 us; the launch traced here: 327 us
  waiting for transfers between devices  169 us (52%)
  blocking collectives  92.7 us (28%)
  matrix products  23.4 us (7%)
  between operations  19.1 us (6%)
  other arithmetic  17.5 us (5%)
  local copies, waits for them, and re-layouts  5.08 us (2%)
    all_gather x1, waiting for transfers between devices, shards(): lax.all_gather(own_cols, 'fsdp', axis=0, tiled=True)  106 us
    all_gather x1, waiting for transfers between devices, shards(): lax.all_gather(hidden, 'tensor', axis=1, tiled=True)  35.7 us
    all_gather x1, waiting for transfers between devices, shards(): pair_rows = lax.all_gather(normed, 'dp', axis=0, tiled=True)  27.3 us
    dot_general x1, matrix products, shards(): jnp.dot(pair_rows, lax.all_gather(own_cols, 'fsdp', axis=0, tiled=True),...  23.4 us
    all_gather x4, blocking collectives, combined_all(): pieces = jax.tree.map(lambda part: lax.all_gather(part, axis), value)  17.4 us
    psum x1, blocking collectives, vocab_stats(): lax.psum((exp_sum, exp_square, picked), 'tensor')  15.5 us
    all_gather x1, blocking collectives, shards(): lax.all_gather(norm_gain, 'tensor', axis=0, tiled=True)  13.6 us
    psum x1, blocking collectives, shards(): lax.psum((jnp.sum(live_mask), jnp.sum(token_loss), jnp.sum(kl_part), jnp....  12.5 us
  transfers between devices with their start and end apart: 3, of which 3 were waited for; matrix products, arithmetic and copies ran while one was open for 2% of the time, Pallas kernels for 0%

commit v1 on v0

--- a/solution.py
+++ b/solution.py
@@ -7,6 +7,14 @@
 kl_coef = 0.2
 log_limit = 10.0
 norm_eps = 1e-06
+
+
+def proceed_regions_over_axis(block_in):
+    current_block = lax.all_to_all(
+        jnp.stack([block_in] * lax.axis_size("fsdp")), split_axis=0, concat_axis=0, axis_name="fsdp"
+    )
+    local_next = jnp.concatenate(current_block, axis=0)
+    return local_next
 
 
 def combined_all(value, axis, join):
@@ -91,9 +99,7 @@
     pair_rows = lax.all_gather(normed, "dp", axis=0, tiled=True)
     pair_ids = lax.all_gather(flat_ids, "dp", axis=0, tiled=True)
     logits = jnp.dot(
-        pair_rows,
-        lax.all_gather(own_cols, "fsdp", axis=0, tiled=True),
-        preferred_element_type=jnp.float32,
+        pair_rows, proceed_regions_over_axis(own_cols), preferred_element_type=jnp.float32
     )
     soft_stats = vocab_stats(logits, pair_ids, tensor_pos * vocab_cols + dp_pos * half_cols)
     soft_stats = combined_all(soft_stats, "dp", join_stats)

time: 328 us -> 347 us (1.058)
  waiting for transfers between devices: 169 us -> 37.5 us
  blocking collectives: 92.7 us -> 211 us
  local copies, waits for them, and re-layouts: 5.08 us -> 29.3 us
  starting transfers between devices: 0.12 us -> 7.14 us
    all_gather x1, blocking collectives: 8.88 us -> 126 us  [shards(): ref_all = lax.all_gather(rollout_logp, ('dp', 'fsdp'), axis=0, tiled=True)]
    all_gather x1 -> x0, waiting for transfers between devices: 106 us -> none  [shards(): lax.all_gather(own_cols, 'fsdp', axis=0, tiled=True)]
    all_gather x1, waiting for transfers between devices: 27.3 us -> 0.01 us  [shards(): pair_rows = lax.all_gather(normed, 'dp', axis=0, tiled=True)]
    all_to_all x0 -> x1, local copies, waits for them, and re-layouts: none -> 20.7 us  [proceed_regions_over_axis(): lax.all_to_all(jnp.stack([block_in] * lax.axis_size('fsdp')), split_axis=...]
    all_to_all x0 -> x1, starting transfers between devices: none -> 7.06 us  [proceed_regions_over_axis(): lax.all_to_all(jnp.stack([block_in] * lax.axis_size('fsdp')), split_axis=...]
    another operation x0 -> x1, local copies, waits for them, and re-layouts: none -> 6.14 us  [proceed_regions_over_axis(): jnp.stack([block_in] * lax.axis_size('fsdp'))]
  transfers between devices with their start and end apart: 3 -> 3, of which waited for: 3 -> 1; matrix products, arithmetic and copies ran while one was open for 2% -> 8% of each run, Pallas kernels for 0% -> 0%
where the time goes in v1:
time: 347 us; the launch traced here: 345 us
  blocking collectives  211 us (61%)
  waiting for transfers between devices  37.5 us (11%)
  local copies, waits for them, and re-layouts  29.3 us (8%)
  matrix products  23.7 us (7%)
  between operations  19.6 us (6%)
  other arithmetic  17.5 us (5%)
  starting transfers between devices  7.14 us (2%)
    all_gather x1, blocking collectives, shards(): ref_all = lax.all_gather(rollout_logp, ('dp', 'fsdp'), axis=0, tiled=True)  126 us
    all_gather x1, waiting for transfers between devices, shards(): lax.all_gather(hidden, 'tensor', axis=1, tiled=True)  36.8 us
    dot_general x1, matrix products, shards(): jnp.dot(pair_rows, proceed_regions_over_axis(own_cols), preferred_element...  23.7 us
    all_to_all x1, local copies, waits for them, and re-layouts, proceed_regions_over_axis(): lax.all_to_all(jnp.stack([block_in] * lax.axis_size('fsdp')), split_axis=...  20.7 us
    all_gather x4, blocking collectives, combined_all(): pieces = jax.tree.map(lambda part: lax.all_gather(part, axis), value)  17.4 us
    psum x1, blocking collectives, vocab_stats(): lax.psum((exp_sum, exp_square, picked), 'tensor')  17.4 us
    all_gather x1, blocking collectives, shards(): lax.all_gather(norm_gain, 'tensor', axis=0, tiled=True)  13.6 us
    psum x1, blocking collectives, shards(): lax.psum((jnp.sum(live_mask), jnp.sum(token_loss), jnp.sum(kl_part), jnp....  12.5 us
  transfers between devices with their start and end apart: 3, of which 1 were waited for; matrix products, arithmetic and copies ran while one was open for 8% of the time, Pallas kernels for 0%

profile of v1, /device:TPU:0, one launch (start us, length us, event | category | flops | bytes accessed | tf_op | source)
XLA Modules:
  0.0 345.5 jit_solution(3509443657696746799)
XLA Ops:
  7.2 2.4 constant_dynamic-slice_fusion.1
  9.6 6.1 %stack.19 = bf16[4,512,4016]{1,2,0:T(8,128)(2,1)} broadcast(bf16[512,4016]{0,1:T(8,128)(2,1)S(1)} %constant_dynamic-slice_fusion.1), dimensions={1,2} | broadcast | bytes 20561920 | tf_op jit(solution)/shard_map/stack | solution.py:14
  15.7 7.1 %all-to-all-start = ((bf16[4,512,4016]{1,2,0:T(8,128)(2,1)}), bf16[4,512,4016]{1,2,0:T(8,128)(2,1)}, u32[]{:S(2)}, u32[]{:S(2)}) async-start(bf16[4,512,4016]{1,2,0:T(8,128)(2,1)} %stack.19), calls=%async_computation | async-start | bytes 32899072 | tf_op jit(solution)/shard_map/all_to_all | solution.py:13
  22.9 0.7 all-gather.10.cloned.1.call-update
  23.6 13.6 %all-gather.2 = bf16[4,1,512]{2,1,0:T(2,128)(2,1)S(1)} all-gather(bf16[1,1,512]{2,1,0:T(2,128)(2,1)S(1)} %reshape.96), channel_id=1, replica_groups=mesh['dp'=2,'fsdp'=4,'tensor'=4] {'tensor'}, dimensions={0}, use_global_device_ids=true | all-gather | bytes 5120 | tf_op jit(solution)/shard_map/all_gather | solution.py:88
  37.3 36.8 %all-gather.10.cloned.1.call-done = bf16[512,2048]{1,0:T(8,128)(2,1)} async-done(((bf16[512,512]{1,0:T(8,128)(2,1)}), bf16[512,2048]{1,0:T(8,128)(2,1)}) %all-gather.10.cloned.1.call-update) | async-done | bytes 2097168 | tf_op jit(solution)/shard_map/all_gather | solution.py:87
  74.1 2.1 fusion.1
  76.1 3.4 fusion.3
  80.9 0.7 convert_reduce_fusion
  81.6 126.1 %all-gather.5 = f32[8,1,128]{2,1,0:T(1,128)S(1)} all-gather(f32[1,1,128]{2,1,0:T(1,128)S(1)} %bitcast.47), channel_id=1, replica_groups=mesh['dp'=2,'fsdp'=4,'tensor'=4] {'dp','fsdp'}, dimensions={0}, use_global_device_ids=true | all-gather | bytes 4608 | tf_op jit(solution)/shard_map/all_gather | solution.py:112
  207.7 11.1 %all_gather.53 = f32[1,512]{1,0:T(1,128)S(1)} all-gather(f32[1,128]{1,0:T(1,128)S(1)} %fusion.8), channel_id=1, replica_groups=mesh['dp'=2,'fsdp'=4,'tensor'=4] {'tensor'}, dimensions={1}, use_global_device_ids=true | all-gather | bytes 2560 | tf_op jit(solution)/shard_map/all_gather | solution.py:114
  218.9 4.4 %all-gather = s32[1,1024]{1,0:T(1,128)S(1)} all-gather(s32[1,512]{1,0:T(1,128)S(1)} %copy-done.1), channel_id=2, replica_groups=mesh['dp'=2,'fsdp'=4,'tensor'=4] {'dp'}, dimensions={1}, use_global_device_ids=true | all-gather | bytes 6144 | tf_op jit(solution)/shard_map/all_gather | solution.py:100
  223.2 20.7 %copy.13 = bf16[4,512,4016]{2,1,0:T(8,128)(2,1)} copy(bf16[4,512,4016]{1,2,0:T(8,128)(2,1)} %all-to-all-done) | data formatting | bytes 32899072 | tf_op jit(solution)/shard_map/all_to_all | solution.py:13
  243.9 23.7 %fusion.15 = (f32[1024]{0:T(1024)S(1)}, f32[1024,4016]{0,1:T(8,128)}) fusion(bf16[1024,2048]{1,0:T(8,128)(2,1)} %all-gather.12.cloned.1.call-done, bf16[2048,4016]{1,0:T(8,128)(2,1)} %bitcast.30), kind=kOutput, calls=%fused_computation.46 | convolution fusion | flops 16848436224 | bytes 37097472 | tf_op jit(solution)/shard_map/dot_general | solution.py:101
  267.6 8.3 %pmax.7 = f32[1024]{0:T(1024)S(1)} all-reduce(f32[1024]{0:T(1024)S(1)} %get-tuple-element.65), channel_id=1, replica_groups=mesh['dp'=2,'fsdp'=4,'tensor'=4] {'tensor'}, use_global_device_ids=true, to_apply=%region_4.5 | all-reduce | flops 1024 | bytes 8192 | tf_op jit(solution)/shard_map/pmax | solution.py:68
  275.9 4.3 %all-gather.1 = f32[2048]{0:T(1024)S(1)} all-gather(f32[1024]{0:T(1024)S(1)} %pmax.7), channel_id=3, replica_groups=mesh['dp'=2,'fsdp'=4,'tensor'=4] {'dp'}, dimensions={0}, use_global_device_ids=true | all-gather | bytes 12288 | tf_op jit(solution)/shard_map/all_gather | solution.py:21
  280.3 8.7 %multiply_reduce_fusion = (f32[1024]{0:T(1024)S(1)}, f32[1024]{0:T(1024)S(1)}, f32[1024]{0:T(1024)S(1)}) fusion(f32[1024,4016]{0,1:T(8,128)} %get-tuple-element.66, f32[1024]{0:T(1024)S(1)} %pmax.7, s32[1024]{0:T(1024)S(1)} %bitcast.35, s32[4016]{0:T(1024)S(1)} %iota_add_fusion), kind=kLoop, calls=%fused_computation | loop fusion | flops 28783616 | bytes 16486080 | tf_op jit(solution)/shard_map/reduce_sum | solution.py:61
  289.0 17.4 %all-reduce.1 = (f32[1,1024]{1,0:T(1,128)S(1)}, f32[1,1024]{1,0:T(1,128)S(1)}, f32[1,1024]{1,0:T(1,128)S(1)}) all-reduce(f32[1,1024]{1,0:T(1,128)S(1)} %bitcast.34, f32[1,1024]{1,0:T(1,128)S(1)} %bitcast.33, f32[1,1024]{1,0:T(1,128)S(1)} %bitcast.32), channel_id=1, replica_groups=mesh['dp'=2,'fsdp'=4,'tensor'=4] {'tensor'}, use_global_device_ids=true, to_apply=%region_2.3 | all-reduce | flops 3072 | bytes 24576 | tf_op jit(solution)/shard_map/psum | solution.py:70
  306.3 4.3 %all-gather.3 = f32[2,1,1024]{2,1,0:T(1,128)S(1)} all-gather(f32[1,1,1024]{2,1,0:T(1,128)S(1)} %bitcast.46), channel_id=1, replica_groups=mesh['dp'=2,'fsdp'=4,'tensor'=4] {'dp'}, dimensions={0}, use_global_device_ids=true | all-gather | bytes 12288 | tf_op jit(solution)/shard_map/all_gather | solution.py:21
  310.7 4.3 %all-gather.6 = f32[2,1,1024]{2,1,0:T(1,128)S(1)} all-gather(f32[1,1,1024]{2,1,0:T(1,128)S(1)} %bitcast.45), channel_id=1, replica_groups=mesh['dp'=2,'fsdp'=4,'tensor'=4] {'dp'}, dimensions={0}, use_global_device_ids=true | all-gather | bytes 12288 | tf_op jit(solution)/shard_map/all_gather | solution.py:21
  315.0 4.3 %all-gather.4 = f32[2,1,1024]{2,1,0:T(1,128)S(1)} all-gather(f32[1,1,1024]{2,1,0:T(1,128)S(1)} %bitcast.44), channel_id=1, replica_groups=mesh['dp'=2,'fsdp'=4,'tensor'=4] {'dp'}, dimensions={0}, use_global_device_ids=true | all-gather | bytes 12288 | tf_op jit(solution)/shard_map/all_gather | solution.py:21
  319.5 1.3 fusion.10
  320.8 0.7 select_reduce_fusion.1
  321.5 12.5 %all-reduce = (f32[]{:T(128)}, f32[]{:T(128)}, f32[]{:T(128)}, f32[]{:T(128)}) all-reduce(f32[]{:T(128)} %get-tuple-element.58, f32[]{:T(128)} %convert_reduce_fusion, f32[]{:T(128)} %select_reduce_fusion.1, f32[]{:T(128)} %get-tuple-element.51), channel_id=1, replica_groups=mesh['dp'=2,'fsdp'=4,'tensor'=4] {'dp','fsdp'}, use_global_device_ids=true, to_apply=%region_16.17 | all-reduce | flops 4 | bytes 32 | tf_op jit(solution)/shard_map/psum | solution.py:120
  (30 shorter events, 0.9 us)
Async XLA Ops:
  15.7 7.9 %copy-start.4 = (bf16[512]{0:T(512)(128)(2,1)S(1)}, bf16[512]{0:T(512)(128)(2,1)}, u32[]{:S(2)}) copy-start(bf16[512]{0:T(512)(128)(2,1)} %param.10) | copy-start | bytes 3076
  15.7 207.5 %all-to-all-start = ((bf16[4,512,4016]{1,2,0:T(8,128)(2,1)}), bf16[4,512,4016]{1,2,0:T(8,128)(2,1)}, u32[]{:S(2)}, u32[]{:S(2)}) async-start(bf16[4,512,4016]{1,2,0:T(8,128)(2,1)} %stack.19), calls=%async_computation | async-start | bytes 32899072 | tf_op jit(solution)/shard_map/all_to_all | solution.py:13
  22.8 58.8 %copy-start.5 = (f32[1,128]{1,0:T(1,128)S(1)}, f32[1,128]{1,0:T(1,128)}, u32[]{:S(2)}) copy-start(f32[1,128]{1,0:T(1,128)} %param.16) | copy-start | bytes 1540
  22.8 196.0 %copy-start.1 = (s32[1,512]{1,0:T(1,128)S(1)}, s32[1,512]{1,0:T(1,128)}, u32[]{:S(2)}) copy-start(s32[1,512]{1,0:T(1,128)} %param.12) | copy-start | bytes 6148
  22.8 51.2 %all-gather.10.cloned.1.call-start = ((), (), s32[]{:S(2)}) async-start(), calls=%async_computation.1 | async-start | bytes 2621440 | tf_op jit(solution)/shard_map/all_gather | solution.py:87
  23.6 220.4 %all-gather.12.cloned.1.call-start = ((), (), s32[]{:S(2)}) async-start(), calls=%async_computation.2 | async-start | bytes 6291456 | tf_op jit(solution)/shard_map/all_gather | solution.py:99
  280.3 39.2 %copy-start.2 = (f32[1,512]{1,0:T(1,128)S(1)}, f32[1,512]{1,0:T(1,128)}, u32[]{:S(2)}) copy-start(f32[1,512]{1,0:T(1,128)} %param.15) | copy-start | bytes 6148
  280.3 39.2 %copy-start.3 = (f32[1,512]{1,0:T(1,128)S(1)}, f32[1,512]{1,0:T(1,128)}, u32[]{:S(2)}) copy-start(f32[1,512]{1,0:T(1,128)} %param.14) | copy-start | bytes 6148
  319.5 19.2 %copy-start = (f32[512]{0:T(512)}, f32[512]{0:T(512)S(1)}, u32[]{:S(2)}) copy-start(f32[512]{0:T(512)S(1)} %get-tuple-element.55) | copy-start | bytes 6148
Sparse Core Ops, SparseCore 0:
  25.2 48.7 all-gather.9
  79.7 55.5 all-gather.11
